TPU v7x, 32 devices: a whole 2x2x4 slice. The times are simulated.
32 devices in a mesh: row: 4 (over z), col: 8 (over y, x, core).
Axes of the slice: x: 2, y: 2, z: 4, core: 2. Of those that a mesh axis runs over, the one named last changes fastest.
Arguments:
- train_points: float32 [4, 32, 4096], P('row', None, 'col'), as said below
- targets: float32 [4, 4096], P('row', 'col'), may hold values from -16 to 16
- inverse_factor: float32 [4, 4096, 1024], P('row', 'col')
- counts: int32 [4, 4], P('row'), may hold values from 512 to 1024, as said below
- membership: int32 [4, 4, 16], replicated, may hold values from 0 to 1, as said below
- test_points: float32 [16, 32, 128], P('row'), may hold values from -6 to 6
Outputs:
- pred_mean: float32 [16, 128], P('row')
- pred_var: float32 [16, 128], P('row')
Inputs may be any that keep to these rules, and one draw needn't show every extreme that they name: Each expert membership[r, c, :] takes part in at least one and at most 4 blocks, exactly 4 for at least one expert, and in at most one of the 4 blocks of each owner row. `counts`: at least one expert has all 1024 points valid. `train_points`: each expert's 1024 points are drawn independently of the other experts' points.
All inputs are finite; a program needn't handle non-finite values.
Results may differ from a plain program's by a relative error of at most 0.0003.
Values sent between devices are 32-bit elements; how exact they have to be, the bound alone decides.
A program may use at most 64 MiB of HBM per device.

v0:
```python
import jax
import jax.numpy as jnp
from jax import lax
from jax.sharding import PartitionSpec as P

SIGNAL = 1.0
NOISE = 0.1
HIGHEST = lax.Precision.HIGHEST


def partner_2(block, axis, distance):
    count = lax.axis_size(axis)
    route = []
    for low in range(count):
        high = low | 1 << distance
        if high != low and high < count:
            route += [(low, high), (high, low)]
    return lax.ppermute(block, axis, route)


def cross_kernel(train_cols, test_cols, squared_scale):
    products = jnp.einsum("dn,dp->np", train_cols, test_cols, precision=HIGHEST)
    spread = (
        jnp.sum(train_cols * train_cols, axis=0)[:, None]
        + jnp.sum(test_cols * test_cols, axis=0)[None, :]
        - 2.0 * products
    )
    return SIGNAL * jnp.exp(-0.5 * spread / squared_scale)


def slot_table(member, slot_count):
    before = jnp.cumsum(member) - member
    slot_ids = jnp.arange(slot_count, dtype=jnp.int32)[:, None]
    picked = ((member[None, :] == 1) & (before[None, :] == slot_ids)).astype(jnp.int32)
    chosen = jnp.sum(picked * jnp.arange(member.shape[0], dtype=jnp.int32)[None, :], axis=1)
    return (picked.astype(jnp.float32), chosen)


def weigh_expert(mean_part, quad_part):
    variance = NOISE + jnp.maximum(SIGNAL - quad_part, 0.0)
    entropy_gap = 0.5 * (jnp.log(SIGNAL + NOISE) - jnp.log(variance))
    weight = entropy_gap / variance
    return (weight * mean_part, weight)


def on_device(train_points, targets, inverse_factor, counts, membership, test_points):
    parity = lax.axis_index("col") % 2
    expert_col = lax.axis_index("col") // 2
    own_row = lax.axis_index("row")
    row_count = lax.axis_size("row")
    slot_count = min(8, row_count)
    features = train_points.shape[1]
    rows_half = train_points.shape[2]
    blocks_own = test_points.shape[0]
    block_len = test_points.shape[2]
    squared_scale = 0.5 * features
    own_points = train_points[0]
    own_targets = targets[0]
    packed = jnp.concatenate([own_points, own_targets[None, :]], axis=0)
    partner = partner_2(packed, "col", 0)
    other_points = partner[:features]
    other_targets = partner[features]
    member = membership[own_row, expert_col]
    picked, chosen = slot_table(member, slot_count)
    wanted = lax.dynamic_slice_in_dim(
        membership[:, expert_col], own_row * blocks_own, blocks_own, 1
    )
    gathered = lax.all_gather(test_points, "row", axis=0, tiled=True)
    slot_tests = gathered[chosen]
    test_cols = slot_tests.transpose(1, 0, 2).reshape(features, slot_count * block_len)
    valid_count = counts[0, expert_col]
    local_index = jnp.arange(rows_half, dtype=jnp.int32)
    own_valid = 2 * local_index + parity < valid_count
    other_valid = 2 * local_index + (1 - parity) < valid_count
    own_kernel = jnp.where(
        own_valid[:, None], cross_kernel(own_points, test_cols, squared_scale), 0.0
    )
    other_kernel = jnp.where(
        other_valid[:, None], cross_kernel(other_points, test_cols, squared_scale), 0.0
    )
    factor_pairs = inverse_factor[0].reshape(rows_half, rows_half, 2)
    own_part = lax.dynamic_index_in_dim(factor_pairs, parity, 2, keepdims=False)
    other_part = lax.dynamic_index_in_dim(factor_pairs, 1 - parity, 2, keepdims=False)
    solved = jnp.dot(own_part, own_kernel, precision=HIGHEST, preferred_element_type=jnp.float32)
    solved = solved + jnp.dot(
        other_part, other_kernel, precision=HIGHEST, preferred_element_type=jnp.float32
    )
    whitened = jnp.dot(own_part, own_targets, precision=HIGHEST, preferred_element_type=jnp.float32)
    whitened = whitened + jnp.dot(
        other_part, other_targets, precision=HIGHEST, preferred_element_type=jnp.float32
    )
    mean_own = jnp.dot(whitened, solved, precision=HIGHEST, preferred_element_type=jnp.float32)
    quad_own = jnp.sum(solved * solved, axis=0)
    partials = partner_2(jnp.stack([mean_own, quad_own], axis=0), "col", 0)
    weighted, weight = weigh_expert(mean_own + partials[0], quad_own + partials[1])
    slot_ids = jnp.arange(slot_count, dtype=jnp.int32)
    my_slots = (slot_ids % 2 == parity).astype(jnp.float32)[:, None]
    my_picked = picked * my_slots
    dense_num = jnp.einsum(
        "sb,sp->bp", my_picked, weighted.reshape(slot_count, block_len), precision=HIGHEST
    )
    dense_wgt = jnp.einsum(
        "sb,sp->bp", my_picked, weight.reshape(slot_count, block_len), precision=HIGHEST
    )
    row_num = jnp.sum(dense_num.reshape(row_count, blocks_own, block_len), axis=1)
    row_wgt = jnp.sum(dense_wgt.reshape(row_count, blocks_own, block_len), axis=1)
    outgoing_sums = jnp.stack([row_num, row_wgt], axis=1)
    arrived = lax.all_to_all(outgoing_sums, "row", split_axis=0, concat_axis=0, tiled=True)
    placed = jnp.einsum("rj,rkp->kjp", wanted.astype(jnp.float32), arrived, precision=HIGHEST)
    total_num, total_wgt = lax.psum((placed[0], placed[1]), "col")
    precision_sum = 1.0 / (SIGNAL + NOISE) + total_wgt
    return (total_num / precision_sum, 1.0 / precision_sum)


def solution(mesh):
    in_specs = (
        P("row", None, "col"),
        P("row", "col"),
        P("row", "col", None),
        P("row", None),
        P(),
        P("row", None, None),
    )
    out_specs = (P("row", None), P("row", None))
    return jax.shard_map(
        on_device, mesh=mesh, in_specs=in_specs, out_specs=out_specs, check_vma=False
    )
```

profile of v0, /device:TPU:0, one launch (start us, length us, event | category | flops | bytes accessed | tf_op | source)
XLA Modules:
  0.0 70.3 jit_solution(5931016102477284509)
XLA Ops:
  0.6 0.9 %pad_maximum_fusion = f32[33,512]{1,0:T(8,128)S(1)} fusion(f32[1,512]{1,0:T(1,128)} %param.7, f32[32,512]{1,0:T(8,128)} %bitcast.99), kind=kLoop, calls=%fused_computation.30 | loop fusion | flops 16896 | bytes 135168 | tf_op jit(solution)/shard_map/concatenate | solution.py:59
  2.0 0.9 %multiply_reduce_fusion.2 = f32[512]{0:T(512)S(1)} fusion(f32[1,32,512]{2,1,0:T(8,128)} %param.6), kind=kLoop, calls=%fused_computation.36 | loop fusion | flops 32256 | bytes 67584 | tf_op jit(solution)/shard_map/reduce_sum | solution.py:24
  2.9 3.0 %copy.30 = f32[1,512,1024]{1,2,0:T(8,128)} copy(f32[1,512,1024]{2,1,0:T(8,128)} %param.8) | data formatting | bytes 4194304 | tf_op args[2]
  5.8 2.5 %reshape_squeeze.3 = f32[512,512,2]{0,2,1:T(2,128)S(1)} reshape(f32[1,512,1024]{1,2,0:T(8,128)} %copy.30) | data formatting | bytes 4194304 | tf_op jit(solution)/shard_map/reshape;squeeze | solution.py:81
  8.3 2.8 %constant_dynamic-slice_fusion = (f32[512,512,1]{0,2,1:T(1,128)}, f32[512,512,1]{0,2,1:T(1,128)S(1)}) fusion(f32[512,512,2]{0,2,1:T(2,128)S(1)} %reshape_squeeze.3, s32[]{:T(128)S(6)} %select_n.68, s32[]{:T(128)S(6)} %select_n.65), kind=kLoop, calls=%fused_computation.76 | loop fusion | bytes 4194312 | tf_op jit(solution)/shard_map/jit(dynamic_index_in_dim)/dynamic_slice | solution.py:83
  11.1 2.4 %copy.34 = f32[512,512,1]{1,0,2:T(8,128)S(1)} copy(f32[512,512,1]{0,2,1:T(1,128)} %get-tuple-element.6) | data formatting | bytes 2097152 | tf_op jit(solution)/shard_map/jit(dynamic_index_in_dim)/dynamic_slice | solution.py:83
  13.5 1.3 %copy.31 = f32[512,512,1]{1,0,2:T(8,128)S(1)} copy(f32[512,512,1]{0,2,1:T(1,128)S(1)} %get-tuple-element.7) | data formatting | bytes 2097152 | tf_op jit(solution)/shard_map/jit(dynamic_index_in_dim)/dynamic_slice | solution.py:82
  14.8 1.0 %fusion.8 = f32[1,512]{1,0:T(1,128)S(1)} fusion(f32[512,512,1]{1,0,2:T(8,128)S(1)} %copy.31, f32[1,512]{1,0:T(1,128)S(1)} %copy-done.3), kind=kOutput, calls=%fused_computation.15 | convolution fusion | flops 3145728 | bytes 1052672 | tf_op jit(solution)/shard_map/dot_general | solution.py:88
  15.8 0.7 %bitcast_compare_fusion = (pred[16]{0:T(512)(128)(4,1)S(1)}, s32[1,1,16]{2,1,0:T(1,128)S(1)}) fusion(s32[4,4,16]{2,1,0:T(4,128)} %param.10, s32[]{:T(128)S(6)} %select_n.60, s32[]{:T(128)S(6)} %select_n.62), kind=kLoop, calls=%fused_computation.83 | loop fusion | flops 16 | bytes 152 | tf_op jit(solution)/shard_map/eq | solution.py:34
  16.9 15.2 %all_gather.3 = f32[16,32,128]{2,1,0:T(8,128)S(1)} all-gather(f32[4,32,128]{2,1,0:T(8,128)S(1)} %copy-done.2), channel_id=1, replica_groups=mesh['row'=4,'col'=8] {'row'}, dimensions={0}, use_global_device_ids=true | all-gather | bytes 327680 | tf_op jit(solution)/shard_map/all_gather | solution.py:68
  33.4 0.7 add_compare_fusion.1
  34.0 1.2 %fusion.4 = f32[512,512]{0,1:T(8,128)S(1)} fusion(f32[512]{0:T(512)S(1)} %bitcast.101, f32[512]{0:T(512)S(1)} %multiply_reduce_fusion.2, pred[512]{0:T(512)(128)(4,1)S(1)} %add_compare_fusion.1, f32[1,32,512]{2,1,0:T(8,128)S(1)} %copy-done.1, f32[4,32,128]{2,1,0:T(8,128)S(1)} %gather_fusion), kind=kOutput, calls=%fused_computation.8 | convolution fusion | flops 101974016 | bytes 1184256 | tf_op jit(solution)/shard_map/dn,dp->np/dot_general | solution.py:22
  35.2 1.9 %fusion.10 = f32[512,512]{1,0:T(8,128)S(1)} fusion(f32[512,512]{0,1:T(8,128)S(1)} %fusion.4, f32[512,512,1]{1,0,2:T(8,128)S(1)} %copy.31), kind=kOutput, calls=%fused_computation.17 | convolution fusion | flops 1610612736 | bytes 3145728 | tf_op jit(solution)/shard_map/dot_general | solution.py:84
  37.6 0.7 reduce.6
  38.4 0.7 add_compare_fusion
  39.1 1.0 %fusion.5 = f32[1,512]{1,0:T(1,128)S(1)} fusion(f32[512,512,1]{1,0,2:T(8,128)S(1)} %copy.34, f32[33,512]{1,0:T(8,128)S(1)} %collective-permute-done), kind=kOutput, calls=%fused_computation.12 | convolution fusion | flops 3145728 | bytes 1052672 | tf_op jit(solution)/shard_map/dot_general | solution.py:89
  40.1 1.0 %convolution_multiply_fusion = f32[512,512]{0,1:T(8,128)S(1)} fusion(f32[33,512]{1,0:T(8,128)S(1)} %collective-permute-done, f32[4,32,128]{2,1,0:T(8,128)S(1)} %gather_fusion), kind=kOutput, calls=%fused_computation.2 | convolution fusion | flops 100925440 | bytes 1179648 | tf_op jit(solution)/shard_map/dn,dp->np/dot_general | solution.py:22
  41.1 2.1 %multiply_reduce_fusion = (f32[512]{0:T(512)S(1)}, f32[512,512]{1,0:T(8,128)S(1)}) fusion(f32[512,512]{1,0:T(8,128)S(1)} %fusion.10, f32[512,512]{0,1:T(8,128)S(1)} %convolution_multiply_fusion, f32[512]{0:T(512)S(1)} %multiply_reduce_fusion.1, f32[512]{0:T(512)S(1)} %bitcast.102, pred[512]{0:T(512)(128)(4,1)S(1)} %add_compare_fusion, ...), kind=kOutput, calls=%fused_computation.19 | convolution fusion | flops 1612447232 | bytes 4200960 | tf_op jit(solution)/shard_map/dot_general | solution.py:85
  44.1 1.1 %collective-permute-done.1 = f32[2,512]{1,0:T(2,128)S(1)} collective-permute-done((f32[2,512]{1,0:T(2,128)S(1)}, f32[2,512]{1,0:T(2,128)S(1)}, u32[]{:S(2)}, u32[]{:S(2)}) %collective-permute-start.1) | collective-permute-done | bytes 4128 | tf_op jit(solution)/shard_map/ppermute | solution.py:18
  45.6 0.6 pad_maximum_fusion.2
  46.3 5.2 %all-to-all-start = ((f32[4,2,128]{2,1,0:T(2,128)}), f32[4,2,128]{2,1,0:T(2,128)S(1)}, u32[]{:S(2)}, u32[]{:S(2)}) async-start(f32[4,2,128]{2,1,0:T(2,128)} %pad_maximum_fusion.2), calls=%async_computation | async-start | bytes 8192 | tf_op jit(solution)/shard_map/all_to_all | solution.py:108
  51.4 0.8 %dynamic-slice_convert_fusion = f32[4,1,4]{2,1,0:T(1,128)S(1)} fusion(s32[4,4,16]{2,1,0:T(4,128)} %param.10, s32[]{:T(128)S(6)} %select_n.70, s32[]{:T(128)S(6)} %select_n.72), kind=kLoop, calls=%fused_computation.62 | loop fusion | flops 16 | bytes 136 | tf_op jit(solution)/shard_map/convert_element_type | solution.py:109
  52.2 4.8 %all-to-all-done = f32[4,2,128]{2,1,0:T(2,128)S(1)} async-done(((f32[4,2,128]{2,1,0:T(2,128)}), f32[4,2,128]{2,1,0:T(2,128)S(1)}, u32[]{:S(2)}, u32[]{:S(2)}) %all-to-all-start) | async-done | bytes 4128 | tf_op jit(solution)/shard_map/all_to_all | solution.py:108
  57.2 12.6 %all-reduce = (f32[4,128]{1,0:T(4,128)S(1)}, f32[4,128]{1,0:T(4,128)S(1)}) all-reduce(f32[4,128]{1,0:T(4,128)S(1)} %get-tuple-element.9, f32[4,128]{1,0:T(4,128)S(1)} %get-tuple-element.8), channel_id=1, replica_groups=mesh['row'=4,'col'=8] {'col'}, use_global_device_ids=true, to_apply=%region_8.9 | all-reduce | flops 1024 | bytes 8192 | tf_op jit(solution)/shard_map/psum | solution.py:110
  (37 shorter events, 4.8 us)
Async XLA Ops:
  0.6 32.1 %copy-start = (s32[1,4]{1,0:T(1,128)S(1)}, s32[1,4]{1,0:T(1,128)}, u32[]{:S(2)}) copy-start(s32[1,4]{1,0:T(1,128)} %param.9) | copy-start | bytes 52
  1.5 37.5 %collective-permute-start = (f32[33,512]{1,0:T(8,128)S(1)}, f32[33,512]{1,0:T(8,128)S(1)}, u32[]{:S(2)}, u32[]{:S(2)}) collective-permute-start(f32[33,512]{1,0:T(8,128)S(1)} %pad_maximum_fusion), channel_id=1, source_target_pairs={{0,1},{1,0},{2,3},{3,2},{4,5},{5,4},{6,7},{7,6},{8,9},{9,8},{10,11... | collective-permute-start | bytes 202760 | tf_op jit(solution)/shard_map/ppermute | solution.py:18
  11.1 3.7 %copy-start.3 = (f32[1,512]{1,0:T(1,128)S(1)}, f32[1,512]{1,0:T(1,128)}, u32[]{:S(2)}) copy-start(f32[1,512]{1,0:T(1,128)} %param.7) | copy-start | bytes 6148
  13.5 3.4 %copy-start.2 = (f32[4,32,128]{2,1,0:T(8,128)S(1)}, f32[4,32,128]{2,1,0:T(8,128)}, u32[]{:S(2)}) copy-start(f32[4,32,128]{2,1,0:T(8,128)} %param.11) | copy-start | bytes 196612
  13.5 20.5 %copy-start.1 = (f32[1,32,512]{2,1,0:T(8,128)S(1)}, f32[1,32,512]{2,1,0:T(8,128)}, u32[]{:S(2)}) copy-start(f32[1,32,512]{2,1,0:T(8,128)} %param.6) | copy-start | bytes 196612
  43.9 1.2 %collective-permute-start.1 = (f32[2,512]{1,0:T(2,128)S(1)}, f32[2,512]{1,0:T(2,128)S(1)}, u32[]{:S(2)}, u32[]{:S(2)}) collective-permute-start(f32[2,512]{1,0:T(2,128)S(1)} %pad_maximum_fusion.1), channel_id=1, source_target_pairs={{0,1},{1,0},{2,3},{3,2},{4,5},{5,4},{6,7},{7,6},{8,9},{9,8},{10,11... | collective-permute-start | bytes 12296 | tf_op jit(solution)/shard_map/ppermute | solution.py:18
  46.3 10.7 %all-to-all-start = ((f32[4,2,128]{2,1,0:T(2,128)}), f32[4,2,128]{2,1,0:T(2,128)S(1)}, u32[]{:S(2)}, u32[]{:S(2)}) async-start(f32[4,2,128]{2,1,0:T(2,128)} %pad_maximum_fusion.2), calls=%async_computation | async-start | bytes 8192 | tf_op jit(solution)/shard_map/all_to_all | solution.py:108
where the time goes:
time: 70.8 us; the launch traced here: 70.3 us
  blocking collectives  27.8 us (39%)
  local copies, waits for them, and re-layouts  13.8 us (19%)
  matrix products  9.53 us (13%)
  other arithmetic  6.76 us (10%)
  waiting for transfers between devices  5.86 us (8%)
  starting transfers between devices  5.72 us (8%)
  between operations  0.83 us (1%)
    all_gather x1, blocking collectives, on_device(): gathered = lax.all_gather(test_points, 'row', axis=0, tiled=True)  15.2 us
    psum x1, blocking collectives, on_device(): total_num, total_wgt = lax.psum((placed[0], placed[1]), 'col')  12.6 us
    all_to_all x1, starting transfers between devices, on_device(): lax.all_to_all(outgoing_sums, 'row', split_axis=0, concat_axis=0, tiled=T...  5.16 us
    dynamic_slice x2, local copies, waits for them, and re-layouts, on_device(): lax.dynamic_index_in_dim(factor_pairs, 1 - parity, 2, keepdims=False)  5.15 us
    all_to_all x1, waiting for transfers between devices, on_device(): lax.all_to_all(outgoing_sums, 'row', split_axis=0, concat_axis=0, tiled=T...  4.81 us
    unnamed x9, local copies, waits for them, and re-layouts  2.98 us
    another operation x1, local copies, waits for them, and re-layouts, on_device(): factor_pairs = inverse_factor[0].reshape(rows_half, rows_half, 2)  2.49 us
    dot_general x2, matrix products, cross_kernel(): products = jnp.einsum('dn,dp->np', train_cols, test_cols, precision=HIGHEST)  2.25 us
  transfers between devices with their start and end apart: 3, of which 2 were waited for; matrix products, arithmetic and copies ran while one was open for 32% of the time, Pallas kernels for 0%

commit v1 on v0

--- a/solution.py
+++ b/solution.py
@@ -65,7 +65,12 @@
     wanted = lax.dynamic_slice_in_dim(
         membership[:, expert_col], own_row * blocks_own, blocks_own, 1
     )
-    gathered = lax.all_gather(test_points, "row", axis=0, tiled=True)
+    ring = [test_points]
+    for hop in range(3):
+        ring.append(lax.ppermute(ring[-1], "row", [(dev, (dev + 1) % 4) for dev in range(4)]))
+    gathered = jnp.roll(
+        jnp.concatenate(ring[::-1], axis=0), (lax.axis_index("row") + 1) * ring[0].shape[0], axis=0
+    )
     slot_tests = gathered[chosen]
     test_cols = slot_tests.transpose(1, 0, 2).reshape(features, slot_count * block_len)
     valid_count = counts[0, expert_col]

time: 70.8 us -> 68.1 us (0.962)
  blocking collectives: 27.8 us -> 12.8 us
  waiting for transfers between devices: 5.86 us -> 15.5 us
  starting transfers between devices: 5.72 us -> 8.06 us
    all_gather x1 -> x0, blocking collectives: 15.2 us -> none  [on_device(): gathered = lax.all_gather(test_points, 'row', axis=0, tiled=True)]
    ppermute x0 -> x3, waiting for transfers between devices: none -> 9.73 us  [on_device(): lax.ppermute(ring[-1], 'row', [(dev, (dev + 1) % 4) for dev in range(4)])]
    ppermute x0 -> x3, starting transfers between devices: none -> 4.74 us  [on_device(): lax.ppermute(ring[-1], 'row', [(dev, (dev + 1) % 4) for dev in range(4)])]
    all_to_all x1, starting transfers between devices: 5.16 us -> 3.24 us  [on_device(): lax.all_to_all(outgoing_sums, 'row', split_axis=0, concat_axis=0, tiled=T...]
    dynamic_slice x2, local copies, waits for them, and re-layouts: 5.15 us -> 4.1 us  [on_device(): lax.dynamic_index_in_dim(factor_pairs, 1 - parity, 2, keepdims=False)]
    dynamic_slice x1, local copies, waits for them, and re-layouts: 1.31 us -> 2.36 us  [on_device(): own_part = lax.dynamic_index_in_dim(factor_pairs, parity, 2, keepdims=False)]
    unnamed x9 -> x16, local copies, waits for them, and re-layouts: 2.98 us -> 3.02 us
  transfers between devices with their start and end apart: 3 -> 6, of which waited for: 2 -> 4; matrix products, arithmetic and copies ran while one was open for 32% -> 31% of each run, Pallas kernels for 0% -> 0%
where the time goes in v1:
time: 68.1 us; the launch traced here: 67.6 us
  waiting for transfers between devices  15.5 us (23%)
  local copies, waits for them, and re-layouts  13.9 us (20%)
  blocking collectives  12.8 us (19%)
  matrix products  9.51 us (14%)
  starting transfers between devices  8.06 us (12%)
  other arithmetic  6.75 us (10%)
  between operations  0.96 us (1%)
    psum x1, blocking collectives, on_device(): total_num, total_wgt = lax.psum((placed[0], placed[1]), 'col')  12.8 us
    ppermute x3, waiting for transfers between devices, on_device(): lax.ppermute(ring[-1], 'row', [(dev, (dev + 1) % 4) for dev in range(4)])  9.73 us
    all_to_all x1, waiting for transfers between devices, on_device(): lax.all_to_all(outgoing_sums, 'row', split_axis=0, concat_axis=0, tiled=T...  4.77 us
    ppermute x3, starting transfers between devices, on_device(): lax.ppermute(ring[-1], 'row', [(dev, (dev + 1) % 4) for dev in range(4)])  4.74 us
    dynamic_slice x2, local copies, waits for them, and re-layouts, on_device(): lax.dynamic_index_in_dim(factor_pairs, 1 - parity, 2, keepdims=False)  4.1 us
    all_to_all x1, starting transfers between devices, on_device(): lax.all_to_all(outgoing_sums, 'row', split_axis=0, concat_axis=0, tiled=T...  3.24 us
    unnamed x16, local copies, waits for them, and re-layouts  3.02 us
    another operation x1, local copies, waits for them, and re-layouts, on_device(): factor_pairs = inverse_factor[0].reshape(rows_half, rows_half, 2)  2.49 us
  transfers between devices with their start and end apart: 6, of which 4 were waited for; matrix products, arithmetic and copies ran while one was open for 31% of the time, Pallas kernels for 0%

profile of v1, /device:TPU:0, one launch (start us, length us, event | category | flops | bytes accessed | tf_op | source)
XLA Modules:
  0.0 67.6 jit_solution(6687823850879580918)
XLA Ops:
  0.6 3.1 %collective-permute-start = (f32[4,32,128]{2,1,0:T(8,128)}, f32[4,32,128]{2,1,0:T(8,128)S(1)}, u32[]{:S(2)}, u32[]{:S(2)}) collective-permute-start(f32[4,32,128]{2,1,0:T(8,128)} %param.11), channel_id=1, source_target_pairs={{0,8},{8,16},{16,24},{24,0},{1,9},{9,17},{17,25},{25,1},{2,10},{10... | collective-permute-start | bytes 196616 | tf_op jit(solution)/shard_map/ppermute | solution.py:70
  3.7 0.9 %pad_maximum_fusion = f32[33,512]{1,0:T(8,128)S(1)} fusion(f32[1,512]{1,0:T(1,128)} %param.7, f32[32,512]{1,0:T(8,128)} %bitcast.99), kind=kLoop, calls=%fused_computation.30 | loop fusion | flops 16896 | bytes 135168 | tf_op jit(solution)/shard_map/concatenate | solution.py:59
  4.7 0.9 %multiply_reduce_fusion.2 = f32[512]{0:T(512)S(1)} fusion(f32[1,32,512]{2,1,0:T(8,128)} %param.6), kind=kLoop, calls=%fused_computation.36 | loop fusion | flops 32256 | bytes 67584 | tf_op jit(solution)/shard_map/reduce_sum | solution.py:24
  5.5 3.0 %copy.30 = f32[1,512,1024]{1,2,0:T(8,128)} copy(f32[1,512,1024]{2,1,0:T(8,128)} %param.8) | data formatting | bytes 4194304 | tf_op args[2]
  8.5 2.5 %reshape_squeeze.3 = f32[512,512,2]{0,2,1:T(2,128)S(1)} reshape(f32[1,512,1024]{1,2,0:T(8,128)} %copy.30) | data formatting | bytes 4194304 | tf_op jit(solution)/shard_map/reshape;squeeze | solution.py:86
  11.0 2.8 %constant_dynamic-slice_fusion = (f32[512,512,1]{0,2,1:T(1,128)S(1)}, f32[512,512,1]{0,2,1:T(1,128)}) fusion(f32[512,512,2]{0,2,1:T(2,128)S(1)} %reshape_squeeze.3, s32[]{:T(128)S(6)} %select_n.82, s32[]{:T(128)S(6)} %select_n.77), kind=kLoop, calls=%fused_computation.84 | loop fusion | bytes 4194312 | tf_op jit(solution)/shard_map/jit(dynamic_index_in_dim)/dynamic_slice | solution.py:88
  13.8 2.4 %copy.31 = f32[512,512,1]{1,0,2:T(8,128)S(1)} copy(f32[512,512,1]{0,2,1:T(1,128)} %get-tuple-element.7) | data formatting | bytes 2097152 | tf_op jit(solution)/shard_map/jit(dynamic_index_in_dim)/dynamic_slice | solution.py:87
  16.2 0.7 %bitcast_compare_fusion = (pred[16]{0:T(512)(128)(4,1)S(1)}, s32[1,1,16]{2,1,0:T(1,128)S(1)}) fusion(s32[4,4,16]{2,1,0:T(4,128)} %param.10, s32[]{:T(128)S(6)} %select_n.72, s32[]{:T(128)S(6)} %select_n.74), kind=kLoop, calls=%fused_computation.92 | loop fusion | flops 16 | bytes 152 | tf_op jit(solution)/shard_map/eq | solution.py:34
  18.5 1.3 %copy.34 = f32[512,512,1]{1,0,2:T(8,128)S(1)} copy(f32[512,512,1]{0,2,1:T(1,128)S(1)} %get-tuple-element.6) | data formatting | bytes 2097152 | tf_op jit(solution)/shard_map/jit(dynamic_index_in_dim)/dynamic_slice | solution.py:88
  19.9 1.0 %fusion.8 = f32[1,512]{1,0:T(1,128)S(1)} fusion(f32[512,512,1]{1,0,2:T(8,128)S(1)} %copy.31, f32[1,512]{1,0:T(1,128)S(1)} %copy-done.3), kind=kOutput, calls=%fused_computation.15 | convolution fusion | flops 3145728 | bytes 1052672 | tf_op jit(solution)/shard_map/dot_general | solution.py:93
  21.4 0.7 reduce.6
  22.8 1.6 %collective-permute-start.1 = (f32[4,32,128]{2,1,0:T(8,128)S(1)}, f32[4,32,128]{2,1,0:T(8,128)S(1)}, u32[]{:S(2)}, u32[]{:S(2)}) collective-permute-start(f32[4,32,128]{2,1,0:T(8,128)S(1)} %collective-permute-done), channel_id=1, source_target_pairs={{0,8},{8,16},{16,24},{24,0},{1,9},{9,17},{17,25},{25,1},{2,10},{10... | collective-permute-start | bytes 196616 | tf_op jit(solution)/shard_map/ppermute | solution.py:70
  24.4 1.0 %fusion.5 = f32[1,512]{1,0:T(1,128)S(1)} fusion(f32[512,512,1]{1,0,2:T(8,128)S(1)} %copy.34, f32[33,512]{1,0:T(8,128)S(1)} %collective-permute-done.3), kind=kOutput, calls=%fused_computation.12 | convolution fusion | flops 3145728 | bytes 1052672 | tf_op jit(solution)/shard_map/dot_general | solution.py:94
  25.4 3.7 %collective-permute-done.1 = f32[4,32,128]{2,1,0:T(8,128)S(1)} collective-permute-done((f32[4,32,128]{2,1,0:T(8,128)S(1)}, f32[4,32,128]{2,1,0:T(8,128)S(1)}, u32[]{:S(2)}, u32[]{:S(2)}) %collective-permute-start.1) | collective-permute-done | bytes 65568 | tf_op jit(solution)/shard_map/ppermute | solution.py:70
  29.1 6.0 %collective-permute-done.2 = f32[4,32,128]{2,1,0:T(8,128)S(1)} collective-permute-done((f32[4,32,128]{2,1,0:T(8,128)S(1)}, f32[4,32,128]{2,1,0:T(8,128)S(1)}, u32[]{:S(2)}, u32[]{:S(2)}) %collective-permute-start.2) | collective-permute-done | bytes 65568 | tf_op jit(solution)/shard_map/ppermute | solution.py:70
  35.9 1.2 %fusion.4 = f32[512,512]{0,1:T(8,128)S(1)} fusion(f32[512]{0:T(512)S(1)} %bitcast.102, f32[512]{0:T(512)S(1)} %multiply_reduce_fusion.2, pred[512]{0:T(512)(128)(4,1)S(1)} %add_compare_fusion.1, f32[1,32,512]{2,1,0:T(8,128)S(1)} %copy-done.1, f32[4,32,128]{2,1,0:T(8,128)S(1)} %gather_fusion), kind=kOutput, calls=%fused_computation.8 | convolution fusion | flops 101974016 | bytes 1184256 | tf_op jit(solution)/shard_map/dn,dp->np/dot_general | solution.py:22
  37.1 1.9 %fusion.10 = f32[512,512]{1,0:T(8,128)S(1)} fusion(f32[512,512]{0,1:T(8,128)S(1)} %fusion.4, f32[512,512,1]{1,0,2:T(8,128)S(1)} %copy.31), kind=kOutput, calls=%fused_computation.17 | convolution fusion | flops 1610612736 | bytes 3145728 | tf_op jit(solution)/shard_map/dot_general | solution.py:89
  39.0 1.0 %convolution_multiply_fusion = f32[512,512]{0,1:T(8,128)S(1)} fusion(f32[33,512]{1,0:T(8,128)S(1)} %collective-permute-done.3, f32[4,32,128]{2,1,0:T(8,128)S(1)} %gather_fusion), kind=kOutput, calls=%fused_computation.2 | convolution fusion | flops 100925440 | bytes 1179648 | tf_op jit(solution)/shard_map/dn,dp->np/dot_general | solution.py:22
  40.0 2.1 %multiply_reduce_fusion = (f32[512]{0:T(512)S(1)}, f32[512,512]{1,0:T(8,128)S(1)}) fusion(f32[512,512]{1,0:T(8,128)S(1)} %fusion.10, f32[512,512]{0,1:T(8,128)S(1)} %convolution_multiply_fusion, f32[512]{0:T(512)S(1)} %multiply_reduce_fusion.1, f32[512]{0:T(512)S(1)} %bitcast.103, pred[512]{0:T(512)(128)(4,1)S(1)} %add_compare_fusion, ...), kind=kOutput, calls=%fused_computation.19 | convolution fusion | flops 1612447232 | bytes 4200960 | tf_op jit(solution)/shard_map/dot_general | solution.py:90
  43.0 1.1 %collective-permute-done.4 = f32[2,512]{1,0:T(2,128)S(1)} collective-permute-done((f32[2,512]{1,0:T(2,128)S(1)}, f32[2,512]{1,0:T(2,128)S(1)}, u32[]{:S(2)}, u32[]{:S(2)}) %collective-permute-start.4) | collective-permute-done | bytes 4128 | tf_op jit(solution)/shard_map/ppermute | solution.py:18
  45.2 3.2 %all-to-all-start = ((f32[4,2,128]{2,1,0:T(2,128)}), f32[4,2,128]{2,1,0:T(2,128)S(1)}, u32[]{:S(2)}, u32[]{:S(2)}) async-start(f32[4,2,128]{2,1,0:T(2,128)} %pad_maximum_fusion.2), calls=%async_computation | async-start | bytes 8192 | tf_op jit(solution)/shard_map/all_to_all | solution.py:113
  48.4 0.8 %dynamic-slice_convert_fusion = f32[4,1,4]{2,1,0:T(1,128)S(1)} fusion(s32[4,4,16]{2,1,0:T(4,128)} %param.10, s32[]{:T(128)S(6)} %select_n.84, s32[]{:T(128)S(6)} %select_n.86), kind=kLoop, calls=%fused_computation.70 | loop fusion | flops 16 | bytes 136 | tf_op jit(solution)/shard_map/convert_element_type | solution.py:114
  49.2 4.8 %all-to-all-done = f32[4,2,128]{2,1,0:T(2,128)S(1)} async-done(((f32[4,2,128]{2,1,0:T(2,128)}), f32[4,2,128]{2,1,0:T(2,128)S(1)}, u32[]{:S(2)}, u32[]{:S(2)}) %all-to-all-start) | async-done | bytes 4128 | tf_op jit(solution)/shard_map/all_to_all | solution.py:113
  54.2 12.8 %all-reduce = (f32[4,128]{1,0:T(4,128)S(1)}, f32[4,128]{1,0:T(4,128)S(1)}) all-reduce(f32[4,128]{1,0:T(4,128)S(1)} %get-tuple-element.9, f32[4,128]{1,0:T(4,128)S(1)} %get-tuple-element.8), channel_id=1, replica_groups=mesh['row'=4,'col'=8] {'col'}, use_global_device_ids=true, to_apply=%region_8.9 | all-reduce | flops 1024 | bytes 8192 | tf_op jit(solution)/shard_map/psum | solution.py:115
  (51 shorter events, 6.3 us)
Async XLA Ops:
  0.6 16.6 %copy-start = (s32[1,4]{1,0:T(1,128)S(1)}, s32[1,4]{1,0:T(1,128)}, u32[]{:S(2)}) copy-start(s32[1,4]{1,0:T(1,128)} %param.9) | copy-start | bytes 52
  0.6 22.1 %collective-permute-start = (f32[4,32,128]{2,1,0:T(8,128)}, f32[4,32,128]{2,1,0:T(8,128)S(1)}, u32[]{:S(2)}, u32[]{:S(2)}) collective-permute-start(f32[4,32,128]{2,1,0:T(8,128)} %param.11), channel_id=1, source_target_pairs={{0,8},{8,16},{16,24},{24,0},{1,9},{9,17},{17,25},{25,1},{2,10},{10... | collective-permute-start | bytes 196616 | tf_op jit(solution)/shard_map/ppermute | solution.py:70
  4.6 19.8 %collective-permute-start.3 = (f32[33,512]{1,0:T(8,128)S(1)}, f32[33,512]{1,0:T(8,128)S(1)}, u32[]{:S(2)}, u32[]{:S(2)}) collective-permute-start(f32[33,512]{1,0:T(8,128)S(1)} %pad_maximum_fusion), channel_id=1, source_target_pairs={{0,1},{1,0},{2,3},{3,2},{4,5},{5,4},{6,7},{7,6},{8,9},{9,8},{10,11... | collective-permute-start | bytes 202760 | tf_op jit(solution)/shard_map/ppermute | solution.py:18
  13.8 6.1 %copy-start.3 = (f32[1,512]{1,0:T(1,128)S(1)}, f32[1,512]{1,0:T(1,128)}, u32[]{:S(2)}) copy-start(f32[1,512]{1,0:T(1,128)} %param.7) | copy-start | bytes 6148
  18.5 16.7 %copy-start.2 = (f32[4,32,128]{2,1,0:T(8,128)S(1)}, f32[4,32,128]{2,1,0:T(8,128)}, u32[]{:S(2)}) copy-start(f32[4,32,128]{2,1,0:T(8,128)} %param.11) | copy-start | bytes 196612
  19.8 16.1 %copy-start.1 = (f32[1,32,512]{2,1,0:T(8,128)S(1)}, f32[1,32,512]{2,1,0:T(8,128)}, u32[]{:S(2)}) copy-start(f32[1,32,512]{2,1,0:T(8,128)} %param.6) | copy-start | bytes 196612
  22.8 6.3 %collective-permute-start.1 = (f32[4,32,128]{2,1,0:T(8,128)S(1)}, f32[4,32,128]{2,1,0:T(8,128)S(1)}, u32[]{:S(2)}, u32[]{:S(2)}) collective-permute-start(f32[4,32,128]{2,1,0:T(8,128)S(1)} %collective-permute-done), channel_id=1, source_target_pairs={{0,8},{8,16},{16,24},{24,0},{1,9},{9,17},{17,25},{25,1},{2,10},{10... | collective-permute-start | bytes 196616 | tf_op jit(solution)/shard_map/ppermute | solution.py:70
  29.1 6.1 %collective-permute-start.2 = (f32[4,32,128]{2,1,0:T(8,128)S(1)}, f32[4,32,128]{2,1,0:T(8,128)S(1)}, u32[]{:S(2)}, u32[]{:S(2)}) collective-permute-start(f32[4,32,128]{2,1,0:T(8,128)S(1)} %collective-permute-done.1), channel_id=1, source_target_pairs={{0,8},{8,16},{16,24},{24,0},{1,9},{9,17},{17,25},{25,1},{2,10},{10... | collective-permute-start | bytes 196616 | tf_op jit(solution)/shard_map/ppermute | solution.py:70
  42.8 1.2 %collective-permute-start.4 = (f32[2,512]{1,0:T(2,128)S(1)}, f32[2,512]{1,0:T(2,128)S(1)}, u32[]{:S(2)}, u32[]{:S(2)}) collective-permute-start(f32[2,512]{1,0:T(2,128)S(1)} %pad_maximum_fusion.1), channel_id=1, source_target_pairs={{0,1},{1,0},{2,3},{3,2},{4,5},{5,4},{6,7},{7,6},{8,9},{9,8},{10,11... | collective-permute-start | bytes 12296 | tf_op jit(solution)/shard_map/ppermute | solution.py:18
  45.2 8.8 %all-to-all-start = ((f32[4,2,128]{2,1,0:T(2,128)}), f32[4,2,128]{2,1,0:T(2,128)S(1)}, u32[]{:S(2)}, u32[]{:S(2)}) async-start(f32[4,2,128]{2,1,0:T(2,128)} %pad_maximum_fusion.2), calls=%async_computation | async-start | bytes 8192 | tf_op jit(solution)/shard_map/all_to_all | solution.py:113
